TPU v7x, 32 devices: a whole 2x2x4 slice. The times are simulated.
32 devices in a mesh: grp: 2 (over y), band: 4 (over x, core), ga: 4 (over z).
Axes of the slice: x: 2, y: 2, z: 4, core: 2. Of those that a mesh axis runs over, the one named last changes fastest.
Arguments:
- orbitals: bfloat16 [64, 8192], P(('grp', 'band'), 'ga'), parts along dimension 0, may hold values from -0.0625 to 0.0625
- energies: float32 [64], P(('grp', 'band')), parts along dimension 0, may hold values from -1.5 to -0.2
- projectors: bfloat16 [1024, 8192], P('grp', 'ga'), parts along dimension 0, may hold values from -0.125 to 0.125
- miller_index: int32 [3, 8192], P(None, 'ga'), may hold values from -12 to 12
- recip_scale: float32 [6], P('grp'), parts along dimension 0, may hold values from 0.06 to 0.14
- species: int32 [128], replicated, may hold values from 0 to 2
- proj_atom: int32 [512], replicated, may hold values from 0 to 127, as said below
- coupling: float32 [3, 4], replicated, may hold values from 0.5 to 3
Outputs:
- response: bfloat16 [3, 64, 8192], P(None, ('grp', 'band'), 'ga'), parts along dimension 1
- dielectric: float32 [6, 3], P('grp'), parts along dimension 0
- born: float32 [9, 256], P(None, 'grp'), parts along dimension 1
There are 2 independent parts, one for each index of `grp`. A program takes and returns all parts, laid end to end along the dimension named above; an argument that names none is the same for every part. Nothing has to cross between parts.
Inputs may be any that keep to these rules, and one draw needn't show every extreme that they name: `proj_atom`: every atom owns exactly 4 projectors.
All inputs are finite; a program needn't handle non-finite values.
Results may differ from a plain program's by a relative error of at most 0.015.
Values may be sent and summed in bfloat16 or wider, within the bound.
A program may use at most 64 MiB of HBM per device.

v0:
```python
import jax
import jax.numpy as jnp
from jax import lax
from jax.sharding import PartitionSpec as P

ITERS = 2
born_scale = 40.0


def tables(miller_index, recip_scale, species, proj_atom, coupling):
    natoms = species.shape[0]
    nspecies = coupling.shape[0]
    nchannels = coupling.shape[1]
    wavevec = miller_index.astype(jnp.float32) * recip_scale[:, None]
    kinetic = 0.5 * jnp.sum(wavevec * wavevec, axis=0)
    atom_onehot = (proj_atom[:, None] == jnp.arange(natoms, dtype=jnp.int32)[None, :]).astype(
        jnp.float32
    )
    spec_proj = jnp.dot(atom_onehot, species.astype(jnp.float32), precision=lax.Precision.HIGHEST)
    spec_onehot = (spec_proj[:, None] == jnp.arange(nspecies, dtype=jnp.float32)[None, :]).astype(
        jnp.float32
    )
    channel = jnp.arange(proj_atom.shape[0], dtype=jnp.int32) % nchannels
    chan_onehot = (channel[:, None] == jnp.arange(nchannels, dtype=jnp.int32)[None, :]).astype(
        jnp.float32
    )
    strength = jnp.sum(
        jnp.dot(spec_onehot, coupling, precision=lax.Precision.HIGHEST) * chan_onehot, axis=1
    )
    return (wavevec, kinetic, atom_onehot, strength)


def per_device(
    orbitals, energies, projectors, miller_index, recip_scale, species, proj_atom, coupling
):
    bands = orbitals.shape[0]
    width = orbitals.shape[1]
    nproj = projectors.shape[0]
    total_bands = bands * lax.axis_size("band")
    wavevec, kinetic, atom_onehot, strength = tables(
        miller_index, recip_scale, species, proj_atom, coupling
    )
    precond = 1.0 / (1.0 + kinetic)

    def conduct(values):
        flat = values.reshape(3 * bands, width)
        block = jnp.dot(
            lax.all_gather(orbitals, "band", axis=0, tiled=True),
            flat.T,
            preferred_element_type=jnp.float32,
        )
        margin = lax.psum(block, "ga").astype(jnp.bfloat16)
        removed = jnp.dot(
            margin.T,
            lax.all_gather(orbitals, "band", axis=0, tiled=True),
            preferred_element_type=jnp.float32,
        )
        return (flat.astype(jnp.float32) - removed).reshape(3, bands, width)

    orb_float = orbitals.astype(jnp.float32)
    stacked = jnp.concatenate([orb_float[None], wavevec[:, None, :] * orb_float[None]], 0).astype(
        jnp.bfloat16
    )
    proj_local = jnp.dot(
        stacked.reshape(4 * bands, width), projectors.T, preferred_element_type=jnp.float32
    )
    proj = lax.psum(proj_local, "ga").reshape(4, bands, nproj)
    weighted = (strength * proj).astype(jnp.bfloat16)
    returned = jnp.dot(
        weighted.reshape(4 * bands, nproj), projectors, preferred_element_type=jnp.float32
    ).reshape(4, bands, width)
    commutator = (wavevec[:, None, :] * (orb_float + returned[0])[None] + returned[1:]).astype(
        jnp.bfloat16
    )
    source = -conduct(commutator)
    response = jnp.zeros_like(source)
    residual = source
    resp_proj = jnp.zeros((3, bands, nproj), jnp.float32)
    diag_shift = kinetic[None, None, :] - energies[None, :, None]
    for step in range(ITERS):
        search = conduct((precond * residual).astype(jnp.bfloat16))
        search_low = search.astype(jnp.bfloat16)
        dir_local = jnp.dot(
            search_low.reshape(3 * bands, width), projectors.T, preferred_element_type=jnp.float32
        )
        num_local = jnp.sum(residual * search, axis=2)
        diag_local = jnp.sum(diag_shift * search * search, axis=2)
        dir_proj, numerator, diag_part = lax.psum((dir_local, num_local, diag_local), "ga")
        dir_proj = dir_proj.reshape(3, bands, nproj)
        dir_weight = (strength * dir_proj).astype(jnp.bfloat16)
        image = diag_shift * search + jnp.dot(
            dir_weight.reshape(3 * bands, nproj), projectors, preferred_element_type=jnp.float32
        ).reshape(3, bands, width)
        curvature = diag_part + jnp.sum(dir_weight.astype(jnp.float32) * dir_proj, axis=2)
        step_size = numerator / curvature
        response = response + step_size[:, :, None] * search
        residual = residual - step_size[:, :, None] * image
        resp_proj = resp_proj + step_size[:, :, None] * dir_proj
    diel_local = jnp.einsum("anx,bnx->ab", response, source, precision=lax.Precision.HIGHEST)
    dielectric = jnp.eye(3, dtype=jnp.float32) + 4.0 / total_bands * lax.psum(
        diel_local, ("band", "ga")
    )
    pair = jnp.einsum("anp,bnp->abp", resp_proj, proj[1:], precision=lax.Precision.HIGHEST)
    born_local = jnp.dot(
        (pair * strength).reshape(9, nproj), atom_onehot, precision=lax.Precision.HIGHEST
    )
    born = born_scale * lax.psum(born_local, "band")
    return (response.astype(jnp.bfloat16), dielectric, born)


def solution(mesh):
    placed = (
        P(("grp", "band"), "ga"),
        P(("grp", "band")),
        P("grp", "ga"),
        P(None, "ga"),
        P("grp"),
        P(),
        P(),
        P(),
    )
    return jax.shard_map(
        per_device,
        mesh=mesh,
        in_specs=placed,
        out_specs=(P(None, ("grp", "band"), "ga"), P("grp", None), P(None, "grp")),
        check_vma=False,
    )
```

profile of v0, /device:TPU:0, one launch (start us, length us, event | category | flops | bytes accessed | tf_op | source)
XLA Modules:
  0.0 192.2 jit_solution(5939086287881664296)
XLA Ops:
  7.3 0.9 convert_element_type.82
  8.2 0.9 multiply_reduce_fusion.3
  9.1 2.1 %fusion.18 = f32[32,512]{1,0:T(8,128)} fusion(bf16[512,2048]{1,0:T(8,128)(2,1)S(1)} %copy-done, bf16[3,8,2048]{2,1,0:T(8,128)(2,1)S(1)} %multiply_convert_fusion.2, bf16[1,8,2048]{2,1,0:T(8,128)(2,1)} %bitcast.93), kind=kOutput, calls=%fused_computation.43 | convolution fusion | flops 67174400 | bytes 2293760 | tf_op jit(solution)/shard_map/dot_general | solution.py:64
  11.3 0.3 fusion.11
  11.7 0.4 fusion.5
  12.0 6.5 %all_gather.2 = bf16[32,2048]{1,0:T(8,128)(2,1)S(1)} all-gather(bf16[8,2048]{1,0:T(8,128)(2,1)S(1)} %copy-done.1), channel_id=1, replica_groups=mesh['grp'=2,'band'=4,'ga'=4] {'band'}, dimensions={0}, use_global_device_ids=true | all-gather | bytes 163840 | tf_op jit(solution)/shard_map/all_gather | solution.py:48
  18.5 29.9 %all-reduce.4.cloned.1.call-done = f32[32,512]{1,0:T(8,128)} async-done(((f32[32,512]{1,0:T(8,128)}), f32[32,512]{1,0:T(8,128)}) %all-reduce.4.cloned.1.call-update) | async-done | bytes 65552 | tf_op jit(solution)/shard_map/psum | solution.py:67
  48.4 1.3 fusion.32
  49.8 0.2 convolution_bitcast_fusion.2
  49.9 17.5 %psum.85 = bf16[32,24]{0,1:T(8,128)(2,1)S(1)} all-reduce(f32[32,24]{0,1:T(8,128)S(1)} %convolution_bitcast_fusion.2), channel_id=1, replica_groups=mesh['grp'=2,'band'=4,'ga'=4] {'ga'}, use_global_device_ids=true, to_apply=%region_2.3 | all-reduce | flops 768 | bytes 4608 | tf_op jit(solution)/shard_map/psum | solution.py:52
  67.6 0.2 convolution_bitcast_fusion.1
  67.7 15.6 %psum.86 = bf16[32,24]{0,1:T(8,128)(2,1)S(1)} all-reduce(f32[32,24]{0,1:T(8,128)S(1)} %convolution_bitcast_fusion.1), channel_id=1, replica_groups=mesh['grp'=2,'band'=4,'ga'=4] {'ga'}, use_global_device_ids=true, to_apply=%region_4.5 | all-reduce | flops 768 | bytes 4608 | tf_op jit(solution)/shard_map/psum | solution.py:52
  83.3 0.3 fusion.13
  83.8 0.7 fusion.27
  84.5 17.3 %all-reduce.1 = (f32[3,8]{1,0:T(4,128)S(1)}, f32[3,8]{1,0:T(4,128)S(1)}, f32[24,512]{1,0:T(8,128)S(1)}) all-reduce(f32[3,8]{1,0:T(4,128)S(1)} %reduce_sum.85, f32[3,8]{1,0:T(4,128)S(1)} %reduce_sum.87, f32[24,512]{1,0:T(8,128)S(1)} %fusion.27), channel_id=1, replica_groups=mesh['grp'=2,'band'=4,'ga'=4] {'ga'}, use_global_device_ids=true, to_apply=%region_6.7 | all-reduce | flops 12336 | bytes 98688 | tf_op jit(solution)/shard_map/psum | solution.py:88
  102.0 0.4 fusion.2
  102.4 0.2 convolution_bitcast_fusion
  102.6 16.5 %psum.90 = bf16[32,24]{0,1:T(8,128)(2,1)S(1)} all-reduce(f32[32,24]{0,1:T(8,128)S(1)} %convolution_bitcast_fusion), channel_id=1, replica_groups=mesh['grp'=2,'band'=4,'ga'=4] {'ga'}, use_global_device_ids=true, to_apply=%region_11.12 | all-reduce | flops 768 | bytes 4608 | tf_op jit(solution)/shard_map/psum | solution.py:52
  119.1 0.2 fusion.15
  119.5 0.7 fusion.25
  120.2 16.3 %all-reduce = (f32[3,8]{1,0:T(4,128)S(1)}, f32[3,8]{1,0:T(4,128)S(1)}, f32[24,512]{1,0:T(8,128)S(1)}) all-reduce(f32[3,8]{1,0:T(4,128)S(1)} %get-tuple-element.16, f32[3,8]{1,0:T(4,128)S(1)} %reduce_sum.92, f32[24,512]{1,0:T(8,128)S(1)} %fusion.25), channel_id=1, replica_groups=mesh['grp'=2,'band'=4,'ga'=4] {'ga'}, use_global_device_ids=true, to_apply=%region_13.14 | all-reduce | flops 12336 | bytes 98688 | tf_op jit(solution)/shard_map/psum | solution.py:88
  136.8 0.7 fusion.17
  137.7 1.4 convolution_bitcast_fusion.3
  139.1 29.7 %psum.94 = f32[3,3]{1,0:T(4,128)S(1)} all-reduce(f32[3,3]{1,0:T(4,128)S(1)} %convolution_bitcast_fusion.3), channel_id=1, replica_groups=mesh['grp'=2,'band'=4,'ga'=4] {'band','ga'}, use_global_device_ids=true, to_apply=%region_18.19 | all-reduce | flops 9 | bytes 72 | tf_op jit(solution)/shard_map/psum | solution.py:100
  168.9 0.6 multiply_add_fusion
  169.5 0.4 copy.25
  169.9 1.3 copy.24
  171.2 5.9 %fusion.4 = f32[3,3,512]{0,1,2:T(4,128)} fusion(f32[3,8,512]{1,0,2:T(4,128)} %copy.24, f32[3,8,512]{1,0,2:T(4,128)S(1)} %copy.25, f32[512]{0:T(512)S(1)} %fusion.5), kind=kOutput, calls=%fused_computation.9 | convolution fusion | flops 446976 | bytes 118784 | tf_op jit(solution)/shard_map/anp,bnp->abp/dot_general | solution.py:103
  177.1 1.6 copy.26
  178.7 0.3 fusion.10
  179.0 5.8 %psum.95 = f32[9,128]{1,0:T(8,128)S(1)} all-reduce(f32[9,128]{1,0:T(8,128)S(1)} %fusion.10), channel_id=1, replica_groups=mesh['grp'=2,'band'=4,'ga'=4] {'band'}, use_global_device_ids=true, to_apply=%region_19.20 | all-reduce | flops 1152 | bytes 9216 | tf_op jit(solution)/shard_map/psum | solution.py:107
  184.8 0.6 broadcast_multiply_fusion
  (38 shorter events, 1.6 us)
Async XLA Ops:
  7.2 1.9 copy-start
  7.2 4.8 %copy-start.1 = (bf16[8,2048]{1,0:T(8,128)(2,1)S(1)}, bf16[8,2048]{1,0:T(8,128)(2,1)}, u32[]{:S(2)}) copy-start(bf16[8,2048]{1,0:T(8,128)(2,1)} %param.8) | copy-start | bytes 98308
  7.2 4.1 %copy-start.5 = (s32[512]{0:T(512)S(1)}, s32[512]{0:T(512)}, u32[]{:S(2)}) copy-start(s32[512]{0:T(512)} %param.14) | copy-start | bytes 6148
  7.2 4.1 %copy-start.6 = (s32[128]{0:T(128)S(1)}, s32[128]{0:T(128)}, u32[]{:S(2)}) copy-start(s32[128]{0:T(128)} %param.13) | copy-start | bytes 1540
  7.2 4.4 %copy-start.3 = (f32[8]{0:T(128)S(1)}, f32[8]{0:T(128)}, u32[]{:S(2)}) copy-start(f32[8]{0:T(128)} %param.9) | copy-start | bytes 100
  7.2 4.4 %copy-start.4 = (f32[3,4]{1,0:T(4,128)S(1)}, f32[3,4]{1,0:T(4,128)}, u32[]{:S(2)}) copy-start(f32[3,4]{1,0:T(4,128)} %param.15) | copy-start | bytes 148
  7.2 41.2 %all-reduce.4.cloned.1.call-start = ((), (), s32[]{:S(2)}) async-start(), calls=%async_computation | async-start | bytes 131072 | tf_op jit(solution)/shard_map/psum | solution.py:67
  119.5 50.4 %copy-start.2 = (f32[32,512]{1,0:T(8,128)S(1)}, f32[32,512]{1,0:T(8,128)}, u32[]{:S(2)}) copy-start(f32[32,512]{1,0:T(8,128)} %all-reduce.4.cloned.1.call-done) | copy-start | bytes 196612
Sparse Core Ops, SparseCore 0:
  11.3 37.0 all-reduce.3
where the time goes:
time: 193 us; the launch traced here: 192 us
  blocking collectives  125 us (65%)
  waiting for transfers between devices  29.9 us (15%)
  matrix products  14.5 us (8%)
  between operations  14.2 us (7%)
  other arithmetic  4.39 us (2%)
  local copies, waits for them, and re-layouts  3.93 us (2%)
    psum x3, blocking collectives, conduct(): margin = lax.psum(block, 'ga').astype(jnp.bfloat16)  49.6 us
    psum x2, blocking collectives, per_device(): lax.psum((dir_local, num_local, diag_local), 'ga')  33.6 us
    psum x1, waiting for transfers between devices, per_device(): proj = lax.psum(proj_local, 'ga').reshape(4, bands, nproj)  29.9 us
    psum x1, blocking collectives, per_device(): lax.psum(diel_local, ('band', 'ga'))  29.7 us
    all_gather x1, blocking collectives, conduct(): lax.all_gather(orbitals, 'band', axis=0, tiled=True)  6.51 us
    dot_general x1, matrix products, per_device(): jnp.einsum('anp,bnp->abp', resp_proj, proj[1:], precision=lax.Precision.H...  5.93 us
    psum x1, blocking collectives, per_device(): born = born_scale * lax.psum(born_local, 'band')  5.77 us
  transfers between devices with their start and end apart: 1, of which 1 were waited for; matrix products, arithmetic and copies ran while one was open for 0% of the time, Pallas kernels for 0%

commit v1 on v0

--- a/solution.py
+++ b/solution.py
@@ -49,7 +49,12 @@
             flat.T,
             preferred_element_type=jnp.float32,
         )
-        margin = lax.psum(block, "ga").astype(jnp.bfloat16)
+
+        def touch_ratios_now(page, ax_name):
+            piece_next = lax.all_gather(page, ax_name)
+            return jnp.sum(piece_next, axis=0)
+
+        margin = touch_ratios_now(block, "ga").astype(jnp.bfloat16)
         removed = jnp.dot(
             margin.T,
             lax.all_gather(orbitals, "band", axis=0, tiled=True),

time: 193 us -> 184 us (0.953)
  blocking collectives: 125 us -> 116 us
    psum x3 -> x0, blocking collectives: 49.6 us -> none  [conduct(): margin = lax.psum(block, 'ga').astype(jnp.bfloat16)]
    all_gather x0 -> x3, blocking collectives: none -> 39.2 us  [touch_ratios_now(): piece_next = lax.all_gather(page, ax_name)]
where the time goes in v1:
time: 184 us; the launch traced here: 183 us
  blocking collectives  116 us (63%)
  waiting for transfers between devices  29.9 us (16%)
  matrix products  14.5 us (8%)
  between operations  14.3 us (8%)
  other arithmetic  4.42 us (2%)
  local copies, waits for them, and re-layouts  3.93 us (2%)
    all_gather x3, blocking collectives, touch_ratios_now(): piece_next = lax.all_gather(page, ax_name)  39.2 us
    psum x2, blocking collectives, per_device(): lax.psum((dir_local, num_local, diag_local), 'ga')  34.9 us
    psum x1, waiting for transfers between devices, per_device(): proj = lax.psum(proj_local, 'ga').reshape(4, bands, nproj)  29.9 us
    psum x1, blocking collectives, per_device(): lax.psum(diel_local, ('band', 'ga'))  29.7 us
    all_gather x1, blocking collectives, conduct(): lax.all_gather(orbitals, 'band', axis=0, tiled=True)  6.51 us
    dot_general x1, matrix products, per_device(): jnp.einsum('anp,bnp->abp', resp_proj, proj[1:], precision=lax.Precision.H...  5.93 us
    psum x1, blocking collectives, per_device(): born = born_scale * lax.psum(born_local, 'band')  5.77 us
  transfers between devices with their start and end apart: 1, of which 1 were waited for; matrix products, arithmetic and copies ran while one was open for 0% of the time, Pallas kernels for 0%

profile of v1, /device:TPU:0, one launch (start us, length us, event | category | flops | bytes accessed | tf_op | source)
XLA Modules:
  0.0 183.1 jit_solution(13177537103049888617)
XLA Ops:
  7.3 0.9 convert_element_type.82
  8.2 0.9 multiply_reduce_fusion.3
  9.1 2.1 %fusion.18 = f32[32,512]{1,0:T(8,128)} fusion(bf16[512,2048]{1,0:T(8,128)(2,1)S(1)} %copy-done, bf16[3,8,2048]{2,1,0:T(8,128)(2,1)S(1)} %multiply_convert_fusion.2, bf16[1,8,2048]{2,1,0:T(8,128)(2,1)} %bitcast.99), kind=kOutput, calls=%fused_computation.43 | convolution fusion | flops 67174400 | bytes 2293760 | tf_op jit(solution)/shard_map/dot_general | solution.py:69
  11.3 0.3 fusion.11
  11.7 0.4 fusion.5
  12.0 6.5 %all_gather.26 = bf16[32,2048]{1,0:T(8,128)(2,1)S(1)} all-gather(bf16[8,2048]{1,0:T(8,128)(2,1)S(1)} %copy-done.1), channel_id=1, replica_groups=mesh['grp'=2,'band'=4,'ga'=4] {'band'}, dimensions={0}, use_global_device_ids=true | all-gather | bytes 163840 | tf_op jit(solution)/shard_map/all_gather | solution.py:48
  18.5 29.9 %all-reduce.4.cloned.1.call-done = f32[32,512]{1,0:T(8,128)} async-done(((f32[32,512]{1,0:T(8,128)}), f32[32,512]{1,0:T(8,128)}) %all-reduce.4.cloned.1.call-update) | async-done | bytes 65552 | tf_op jit(solution)/shard_map/psum | solution.py:72
  48.4 1.3 fusion.32
  49.8 0.2 convolution_bitcast_fusion.2
  49.9 13.1 %all-gather.3 = f32[4,32,24]{1,2,0:T(8,128)S(1)} all-gather(f32[1,32,24]{1,2,0:T(8,128)S(1)} %convolution_bitcast_fusion.2), channel_id=2, replica_groups=mesh['grp'=2,'band'=4,'ga'=4] {'ga'}, dimensions={0}, use_global_device_ids=true | all-gather | bytes 15360 | tf_op jit(solution)/shard_map/all_gather | solution.py:54
  63.2 0.2 convolution_bitcast_fusion.1
  63.3 13.1 %all-gather.4 = f32[4,32,24]{1,2,0:T(8,128)S(1)} all-gather(f32[1,32,24]{1,2,0:T(8,128)S(1)} %convolution_bitcast_fusion.1), channel_id=3, replica_groups=mesh['grp'=2,'band'=4,'ga'=4] {'ga'}, dimensions={0}, use_global_device_ids=true | all-gather | bytes 15360 | tf_op jit(solution)/shard_map/all_gather | solution.py:54
  76.4 0.3 fusion.13
  76.9 0.7 fusion.27
  77.5 18.4 %all-reduce.1 = (f32[3,8]{1,0:T(4,128)S(1)}, f32[3,8]{1,0:T(4,128)S(1)}, f32[24,512]{1,0:T(8,128)S(1)}) all-reduce(f32[3,8]{1,0:T(4,128)S(1)} %reduce_sum.114, f32[3,8]{1,0:T(4,128)S(1)} %reduce_sum.116, f32[24,512]{1,0:T(8,128)S(1)} %fusion.27), channel_id=1, replica_groups=mesh['grp'=2,'band'=4,'ga'=4] {'ga'}, use_global_device_ids=true, to_apply=%region_6.7 | all-reduce | flops 12336 | bytes 98688 | tf_op jit(solution)/shard_map/psum | solution.py:93
  96.3 0.4 fusion.2
  96.7 0.2 convolution_bitcast_fusion
  96.8 13.1 %all-gather.5 = f32[4,32,24]{1,2,0:T(8,128)S(1)} all-gather(f32[1,32,24]{1,2,0:T(8,128)S(1)} %convolution_bitcast_fusion), channel_id=4, replica_groups=mesh['grp'=2,'band'=4,'ga'=4] {'ga'}, dimensions={0}, use_global_device_ids=true | all-gather | bytes 15360 | tf_op jit(solution)/shard_map/all_gather | solution.py:54
  109.9 0.2 fusion.15
  110.3 0.7 fusion.25
  111.1 16.4 %all-reduce = (f32[3,8]{1,0:T(4,128)S(1)}, f32[3,8]{1,0:T(4,128)S(1)}, f32[24,512]{1,0:T(8,128)S(1)}) all-reduce(f32[3,8]{1,0:T(4,128)S(1)} %get-tuple-element.16, f32[3,8]{1,0:T(4,128)S(1)} %reduce_sum.122, f32[24,512]{1,0:T(8,128)S(1)} %fusion.25), channel_id=1, replica_groups=mesh['grp'=2,'band'=4,'ga'=4] {'ga'}, use_global_device_ids=true, to_apply=%region_13.14 | all-reduce | flops 12336 | bytes 98688 | tf_op jit(solution)/shard_map/psum | solution.py:93
  127.8 0.7 fusion.17
  128.6 1.4 convolution_bitcast_fusion.3
  130.1 29.7 %psum.70 = f32[3,3]{1,0:T(4,128)S(1)} all-reduce(f32[3,3]{1,0:T(4,128)S(1)} %convolution_bitcast_fusion.3), channel_id=1, replica_groups=mesh['grp'=2,'band'=4,'ga'=4] {'band','ga'}, use_global_device_ids=true, to_apply=%region_18.19 | all-reduce | flops 9 | bytes 72 | tf_op jit(solution)/shard_map/psum | solution.py:105
  159.8 0.6 multiply_add_fusion
  160.4 0.4 copy.31
  160.8 1.3 copy.30
  162.1 5.9 %fusion.4 = f32[3,3,512]{0,1,2:T(4,128)} fusion(f32[3,8,512]{1,0,2:T(4,128)} %copy.30, f32[3,8,512]{1,0,2:T(4,128)S(1)} %copy.31, f32[512]{0:T(512)S(1)} %fusion.5), kind=kOutput, calls=%fused_computation.9 | convolution fusion | flops 446976 | bytes 118784 | tf_op jit(solution)/shard_map/anp,bnp->abp/dot_general | solution.py:108
  168.0 1.6 copy.32
  169.6 0.3 fusion.10
  169.9 5.8 %psum.71 = f32[9,128]{1,0:T(8,128)S(1)} all-reduce(f32[9,128]{1,0:T(8,128)S(1)} %fusion.10), channel_id=1, replica_groups=mesh['grp'=2,'band'=4,'ga'=4] {'band'}, use_global_device_ids=true, to_apply=%region_19.20 | all-reduce | flops 1152 | bytes 9216 | tf_op jit(solution)/shard_map/psum | solution.py:112
  175.7 0.6 broadcast_multiply_fusion
  (41 shorter events, 1.6 us)
Async XLA Ops:
  7.2 1.9 %copy-start = (bf16[512,2048]{1,0:T(8,128)(2,1)S(1)}, bf16[512,2048]{1,0:T(8,128)(2,1)}, u32[]{:S(2)}) copy-start(bf16[512,2048]{1,0:T(8,128)(2,1)} %param.10) | copy-start | bytes 6291460
  7.2 4.8 %copy-start.1 = (bf16[8,2048]{1,0:T(8,128)(2,1)S(1)}, bf16[8,2048]{1,0:T(8,128)(2,1)}, u32[]{:S(2)}) copy-start(bf16[8,2048]{1,0:T(8,128)(2,1)} %param.8) | copy-start | bytes 98308
  7.2 4.1 %copy-start.5 = (s32[512]{0:T(512)S(1)}, s32[512]{0:T(512)}, u32[]{:S(2)}) copy-start(s32[512]{0:T(512)} %param.14) | copy-start | bytes 6148
  7.2 4.1 %copy-start.6 = (s32[128]{0:T(128)S(1)}, s32[128]{0:T(128)}, u32[]{:S(2)}) copy-start(s32[128]{0:T(128)} %param.13) | copy-start | bytes 1540
  7.2 4.4 %copy-start.3 = (f32[8]{0:T(128)S(1)}, f32[8]{0:T(128)}, u32[]{:S(2)}) copy-start(f32[8]{0:T(128)} %param.9) | copy-start | bytes 100
  7.2 4.4 %copy-start.4 = (f32[3,4]{1,0:T(4,128)S(1)}, f32[3,4]{1,0:T(4,128)}, u32[]{:S(2)}) copy-start(f32[3,4]{1,0:T(4,128)} %param.15) | copy-start | bytes 148
  7.2 41.2 %all-reduce.4.cloned.1.call-start = ((), (), s32[]{:S(2)}) async-start(), calls=%async_computation | async-start | bytes 131072 | tf_op jit(solution)/shard_map/psum | solution.py:72
  110.3 50.4 %copy-start.2 = (f32[32,512]{1,0:T(8,128)S(1)}, f32[32,512]{1,0:T(8,128)}, u32[]{:S(2)}) copy-start(f32[32,512]{1,0:T(8,128)} %all-reduce.4.cloned.1.call-done) | copy-start | bytes 196612
Sparse Core Ops, SparseCore 0:
  11.3 37.0 all-reduce.3
